TPU v7x, 32 devices: a whole 2x2x4 slice. The times are simulated.
32 devices in a mesh: rep: 2 (over x), emb: 4 (over z), model: 4 (over y, core).
Axes of the slice: x: 2, y: 2, z: 4, core: 2. Of those that a mesh axis runs over, the one named last changes fastest.
Arguments:
- x: bfloat16 [1024, 2048], P('rep'), parts along dimension 0
- Wq: bfloat16 [2048, 2048], P('emb', 'model')
- Wk: bfloat16 [2048, 256], replicated
- Wv: bfloat16 [2048, 256], replicated
- Wo: bfloat16 [2048, 2048], P('model', 'emb')
- Kc: bfloat16 [1024, 1024, 256], P('rep'), parts along dimension 0
- Vc: bfloat16 [1024, 1024, 256], P('rep'), parts along dimension 0
- lengths: int32 [1024], P('rep'), parts along dimension 0
Outputs:
- output 1: bfloat16 [1024, 2048], P('rep'), parts along dimension 0
- output 2: bfloat16 [1024, 256], P('rep'), parts along dimension 0
- output 3: bfloat16 [1024, 256], P('rep'), parts along dimension 0
There are 2 independent parts. A program takes and returns all parts, laid end to end along the dimension named above; an argument that names none is the same for every part.
All inputs are finite; a program needn't handle non-finite values.
Results may differ from a plain program's by a relative error of at most 0.0109362.
Values are sent between devices in bfloat16 or wider.
A program may use at most 2.25 GiB of HBM per device.

v0:
```python
import jax
import jax.numpy as jnp
from jax import lax
from jax.sharding import PartitionSpec as P


def _attend(q, K, V, kn, vn, lens):
    dh = q.shape[-1]
    t = K.shape[1]
    scale = dh ** -0.5
    s = jnp.einsum('bhd,btd->bht', q, K, preferred_element_type=jnp.float32) * scale
    valid = jnp.arange(t)[None, :] < lens[:, None]
    s = jnp.where(valid[:, None, :], s, -jnp.inf)
    sn = jnp.einsum('bhd,bd->bh', q, kn, preferred_element_type=jnp.float32) * scale
    m = jnp.maximum(jnp.max(s, axis=-1), sn)
    p = jnp.exp(s - m[..., None])
    pn = jnp.exp(sn - m)
    l = jnp.sum(p, axis=-1) + pn
    acc = jnp.einsum('bht,btd->bhd', p.astype(jnp.bfloat16), V, preferred_element_type=jnp.float32)
    acc = acc + pn.astype(jnp.bfloat16).astype(jnp.float32)[..., None] * vn.astype(jnp.float32)[:, None, :]
    return (acc / l[..., None]).astype(jnp.bfloat16)


def solution(mesh):
    ne = mesh.shape['emb']
    nm = mesh.shape['model']

    def local(x, Wq, Wk, Wv, Wo, Kc, Vc, lengths):
        b, d = x.shape
        de = Wq.shape[0]
        dh = Wk.shape[1]
        hl = Wq.shape[1] // dh
        be = b // ne
        bl = be // nm
        i = lax.axis_index('emb')
        j = lax.axis_index('model')
        xi = lax.dynamic_slice_in_dim(x, i * de, de, axis=1)
        qp = jnp.dot(xi, Wq, preferred_element_type=jnp.float32)
        q = lax.psum_scatter(qp, 'emb', scatter_dimension=0, tiled=True)
        q = q.astype(jnp.bfloat16).reshape(be, hl, dh)
        q = lax.all_to_all(q, 'model', 0, 1, tiled=True)
        k_new = jnp.dot(x, Wk, preferred_element_type=jnp.float32).astype(jnp.bfloat16)
        v_new = jnp.dot(x, Wv, preferred_element_type=jnp.float32).astype(jnp.bfloat16)
        start = i * be + j * bl
        K = lax.dynamic_slice_in_dim(Kc, start, bl, 0)
        V = lax.dynamic_slice_in_dim(Vc, start, bl, 0)
        kn = lax.dynamic_slice_in_dim(k_new, start, bl, 0)
        vn = lax.dynamic_slice_in_dim(v_new, start, bl, 0)
        lens = lax.dynamic_slice_in_dim(lengths, start, bl, 0)
        o = _attend(q, K, V, kn, vn, lens)
        o = lax.all_to_all(o, 'model', 1, 0, tiled=True)
        o = lax.all_gather(o, 'emb', axis=0, tiled=True)
        yp = jnp.dot(o.reshape(b, hl * dh), Wo, preferred_element_type=jnp.float32).astype(jnp.bfloat16)
        ys = lax.psum(yp, 'model')
        yi = (xi.astype(jnp.float32) + ys.astype(jnp.float32)).astype(jnp.bfloat16)
        y = lax.all_gather(yi, 'emb', axis=1, tiled=True)
        return y, k_new, v_new

    in_specs = (P('rep', None), P('emb', 'model'), P(), P(), P('model', 'emb'),
                P('rep', None, None), P('rep', None, None), P('rep'))
    out_specs = (P('rep', None), P('rep', None), P('rep', None))
    return jax.shard_map(local, mesh=mesh, in_specs=in_specs, out_specs=out_specs, check_vma=False)
```

profile of v0, /device:TPU:1, one launch (start us, length us, event | category | flops | bytes accessed | tf_op | source)
XLA Modules:
  0.0 180.7 jit_solution(10689360637297215479)
XLA Ops:
  7.2 0.0 copy-start
  7.2 0.0 reduce-scatter.2.cloned.1.call-start
  7.2 2.8 %fusion.23 = f32[512,512]{1,0:T(8,128)} fusion(bf16[512,512]{1,0:T(8,128)(2,1)} %param.9, bf16[512,2048]{1,0:T(8,128)(2,1)} %param.8, s32[]{:T(128)S(6)} %select_n.14), kind=kOutput, calls=%fused_computation.17 | convolution fusion | flops 268435456 | bytes 2097156 | tf_op jit(solution)/shard_map/dot_general | solution.py:38
  10.0 0.0 reduce-scatter.2.cloned.1.call-update
  10.1 0.8 dynamic_slice.19
  10.9 0.7 convolution_convert_fusion.1
  11.6 0.0 copy-start.2
  11.7 0.1 iota_compare_fusion
  11.8 1.4 convolution_convert_fusion.2
  13.2 26.2 %reduce-scatter.2.cloned.1.call-done = f32[128,512]{1,0:T(8,128)} async-done(((f32[512,512]{1,0:T(8,128)}), f32[128,512]{1,0:T(8,128)}) %reduce-scatter.2.cloned.1.call-update) | async-done | bytes 262160 | tf_op jit(solution)/shard_map/reduce_scatter | solution.py:39
  39.4 1.0 convert_element_type.37
  40.4 0.7 reshape.33
  41.1 4.8 %all-to-all-start = ((bf16[128,2,256]{2,1,0:T(2,128)(2,1)}), bf16[128,2,256]{2,1,0:T(2,128)(2,1)S(1)}, u32[]{:S(2)}, u32[]{:S(2)}) async-start(bf16[128,2,256]{2,1,0:T(2,128)(2,1)} %reshape.33), calls=%async_computation.1 | async-start | bytes 262144 | tf_op jit(solution)/shard_map/all_to_all | solution.py:41
  45.9 0.7 dynamic-slice_bitcast_fusion
  46.6 2.6 %all-to-all-done = bf16[128,2,256]{2,1,0:T(2,128)(2,1)S(1)} async-done(((bf16[128,2,256]{2,1,0:T(2,128)(2,1)}), bf16[128,2,256]{2,1,0:T(2,128)(2,1)S(1)}, u32[]{:S(2)}, u32[]{:S(2)}) %all-to-all-start) | async-done | bytes 131104 | tf_op jit(solution)/shard_map/all_to_all | solution.py:41
  49.3 0.1 copy.29
  49.4 0.1 all_to_all.29
  49.4 0.1 fusion.25
  49.6 10.3 %fusion.31 = (f32[32,8]{1,0:T(8,128)S(1)}, f32[32,8,1024]{2,1,0:T(8,128)S(1)}) fusion(bf16[32,8,256]{2,1,0:T(8,128)(2,1)S(1)} %all_to_all.29, bf16[512,1024,256]{2,1,0:T(8,128)(2,1)} %param.13, s32[]{:T(128)S(6)} %select_n.15, pred[32,1024]{1,0:T(8,128)(4,1)S(1)} %iota_compare_fusion), kind=kOutput, calls=%fused_computation.32 | convolution fusion | flops 135003904 | bytes 17990660 | tf_op jit(solution)/shard_map/bhd,btd->bht/dot_general | solution.py:11
  59.9 0.3 fusion.19
  60.2 8.1 %fusion.16 = bf16[32,8,256]{2,1,0:T(8,128)(2,1)S(1)} fusion(bf16[512,1024,256]{2,1,0:T(8,128)(2,1)} %param.14, s32[]{:T(128)S(6)} %select_n.15, f32[32,8,1024]{2,1,0:T(8,128)S(1)} %get-tuple-element.6, f32[32,8]{1,0:T(8,128)S(1)} %multiply_maximum_fusion, f32[32,8]{1,0:T(8,128)S(1)} %get-tuple-element.4, f32[32,256]{1,0:T(8,128)S(1)} %dynamic-slice_convert_fusion, ...), kind=kOutput, calls=%fused_computation.11 | convolution fusion | flops 135004160 | bytes 17992708 | tf_op jit(solution)/shard_map/bht,btd->bhd/dot_general | solution.py:19
  68.4 7.1 %all_to_all.36 = bf16[32,8,256]{2,0,1:T(8,128)(2,1)S(1)} all-to-all(bf16[32,8,256]{2,0,1:T(8,128)(2,1)S(1)} %copy.21), channel_id=1, replica_groups=mesh['rep'=2,'emb'=4,'model'=4] {'model'}, dimensions={1} | all-to-all | bytes 262144 | tf_op jit(solution)/shard_map/all_to_all | solution.py:51
  75.5 11.8 %all_gather.6 = bf16[512,2,256]{2,0,1:T(8,128)(2,1)S(1)} all-gather(bf16[128,2,256]{2,0,1:T(8,128)(2,1)S(1)} %bitcast.22), channel_id=1, replica_groups=mesh['rep'=2,'emb'=4,'model'=4] {'emb'}, dimensions={0}, use_global_device_ids=true | all-gather | bytes 655360 | tf_op jit(solution)/shard_map/all_gather | solution.py:52
  87.3 0.2 copy.23
  87.5 1.3 convolution_convert_fusion
  88.8 0.0 all-reduce.2.cloned.1.call-update
  88.8 0.0 all-gather.2.cloned.1.call-start
  88.9 33.8 %all-reduce.2.cloned.1.call-done = bf16[512,512]{1,0:T(8,128)(2,1)} async-done(((bf16[512,512]{1,0:T(8,128)(2,1)}), bf16[512,512]{1,0:T(8,128)(2,1)}) %all-reduce.2.cloned.1.call-update) | async-done | bytes 524304 | tf_op jit(solution)/shard_map/psum | solution.py:54
  122.6 2.1 %add_convert_fusion = bf16[512,512]{1,0:T(8,128)(2,1)} fusion(bf16[512,512]{1,0:T(8,128)(2,1)} %all-reduce.2.cloned.1.call-done, bf16[512,2048]{1,0:T(8,128)(2,1)} %param.8, s32[]{:T(128)S(6)} %select_n.14), kind=kLoop, calls=%fused_computation.12 | loop fusion | flops 1048576 | bytes 1572868 | tf_op jit(solution)/shard_map/convert_element_type | solution.py:55
  124.8 0.0 all-gather.2.cloned.1.call-update
  124.8 46.2 %all-gather.2.cloned.1.call-done = bf16[512,2048]{1,0:T(8,128)(2,1)} async-done(((bf16[512,512]{1,0:T(8,128)(2,1)}), bf16[512,2048]{1,0:T(8,128)(2,1)}) %all-gather.2.cloned.1.call-update) | async-done | bytes 2097168 | tf_op jit(solution)/shard_map/all_gather | solution.py:56
  171.0 3.2 %copy.32 = bf16[512,2048]{1,0:T(8,128)(2,1)} copy(bf16[512,2048]{1,0:T(8,128)(2,1)} %all-gather.2.cloned.1.call-done) | data formatting | bytes 4194304
  (14 shorter events, 0.1 us)
Async XLA Ops:
  7.2 3.7 %copy-start = (bf16[2048,256]{1,0:T(8,128)(2,1)S(1)}, bf16[2048,256]{1,0:T(8,128)(2,1)}, u32[]{:S(2)}) copy-start(bf16[2048,256]{1,0:T(8,128)(2,1)} %param.11) | copy-start | bytes 3145732
  7.2 3.7 %copy-start.1 = (bf16[512,2048]{1,0:T(8,128)(2,1)S(1)}, bf16[512,2048]{1,0:T(8,128)(2,1)}, u32[]{:S(2)}) copy-start(bf16[512,2048]{1,0:T(8,128)(2,1)} %param.8) | copy-start | bytes 6291460
  7.2 32.2 %reduce-scatter.2.cloned.1.call-start = ((), (), s32[]{:S(2)}) async-start(), calls=%async_computation.3 | async-start | bytes 1310720 | tf_op jit(solution)/shard_map/reduce_scatter | solution.py:39
  10.0 1.7 copy-start.3
  11.6 28.8 %copy-start.2 = (bf16[512,256]{1,0:T(8,128)(2,1)}, bf16[512,256]{1,0:T(8,128)(2,1)S(1)}, u32[]{:S(2)}) copy-start(bf16[512,256]{1,0:T(8,128)(2,1)S(1)} %convolution_convert_fusion.1) | copy-start | bytes 786436
  41.1 8.2 %all-to-all-start = ((bf16[128,2,256]{2,1,0:T(2,128)(2,1)}), bf16[128,2,256]{2,1,0:T(2,128)(2,1)S(1)}, u32[]{:S(2)}, u32[]{:S(2)}) async-start(bf16[128,2,256]{2,1,0:T(2,128)(2,1)} %reshape.33), calls=%async_computation.1 | async-start | bytes 262144 | tf_op jit(solution)/shard_map/all_to_all | solution.py:41
  45.9 76.7 %all-reduce.2.cloned.1.call-start = ((), (), s32[]{:S(2)}) async-start(), calls=%async_computation.4 | async-start | bytes 1048576 | tf_op jit(solution)/shard_map/psum | solution.py:54
  68.3 19.2 %copy-start.4 = (bf16[512,512]{1,0:T(8,128)(2,1)S(1)}, bf16[512,512]{1,0:T(8,128)(2,1)}, u32[]{:S(2)}) copy-start(bf16[512,512]{1,0:T(8,128)(2,1)} %param.12) | copy-start | bytes 1572868
  88.8 82.2 %all-gather.2.cloned.1.call-start = ((), (), s32[]{:S(2)}) async-start(), calls=%async_computation.5 | async-start | bytes 2621440 | tf_op jit(solution)/shard_map/all_gather | solution.py:56
Sparse Core Ops, SparseCore 0:
  10.9 28.5 reduce-scatter.1
  88.9 33.6 all-reduce.1
  124.9 46.0 all-gather.1
where the time goes:
time: 183 us; the launch traced here: 181 us
  waiting for transfers between devices  109 us (60%)
  matrix products  24.7 us (13%)
  blocking collectives  18.9 us (10%)
  between operations  13.9 us (8%)
  local copies, waits for them, and re-layouts  5.84 us (3%)
  starting transfers between devices  4.91 us (3%)
  other arithmetic  3.53 us (2%)
    all_gather x1, waiting for transfers between devices, local(): y = lax.all_gather(yi, 'emb', axis=1, tiled=True)  46.2 us
    psum x1, waiting for transfers between devices, local(): ys = lax.psum(yp, 'model')  33.8 us
    reduce_scatter x1, waiting for transfers between devices, local(): q = lax.psum_scatter(qp, 'emb', scatter_dimension=0, tiled=True)  26.2 us
    all_gather x1, blocking collectives, local(): o = lax.all_gather(o, 'emb', axis=0, tiled=True)  11.8 us
    dot_general x1, matrix products, _attend(): jnp.einsum('bhd,btd->bht', q, K, preferred_element_type=jnp.float32) * scale  10.3 us
    dot_general x1, matrix products, _attend(): jnp.einsum('bht,btd->bhd', p.astype(jnp.bfloat16), V, preferred_element_t...  8.14 us
    all_to_all x1, blocking collectives, local(): o = lax.all_to_all(o, 'model', 1, 0, tiled=True)  7.12 us
    all_to_all x1, starting transfers between devices, local(): q = lax.all_to_all(q, 'model', 0, 1, tiled=True)  4.82 us
  transfers between devices with their start and end apart: 4, of which 4 were waited for; matrix products, arithmetic and copies ran while one was open for 2% of the time, Pallas kernels for 0%

commit v1 on v0

v1 whole, which is shorter than its diff:
```python
import functools

import jax
import jax.numpy as jnp
from jax import lax
from jax.experimental import pallas as pl
from jax.experimental.pallas import tpu as pltpu
from jax.sharding import PartitionSpec as P

BF = jnp.bfloat16
F32 = jnp.float32
NB = 2
UNROLL = 4
CHUNK = 8


def _kernel(x_h, wq_h, wk_h, wv_h, wo_h, kc_h, vc_h, lens,
            y_h, kn_h, vn_h,
            x_v, wq_v, wall, wk_v, wv_v, wo_v, k_v, v_v, kn_v, vn_v, knf, vnf,
            qacc, q_my, q_in, qf, of, o_in, y_v,
            lsem, ksem, vsem, osem,
            a_s, a_r, x_s, x_r, c_s, c_r, w_s, w_r, o_s, o_r,
            yz_s, yz_r, yy_s, yy_r, yd_s, yd_r):
    r = lax.axis_index('rep')
    z = lax.axis_index('emb')
    m = lax.axis_index('model')
    yy = m // 2
    c = m % 2
    my = yy * 2 + 1 - c
    mx = (1 - yy) * 2 + c
    me = z * 4 + m
    bl = k_v.shape[0]
    nb = bl // NB
    t = k_v.shape[1]
    dh = k_v.shape[2]
    nh = 8
    half = dh // 2
    de = wq_v.shape[0]
    hr = de // 2
    start = pl.multiple_of(me * bl, bl)
    scale = dh ** -0.5

    def rcopy(src, dst, ss, rs, rr, zz, mm):
        return pltpu.make_async_remote_copy(
            src_ref=src, dst_ref=dst, send_sem=ss, recv_sem=rs,
            device_id=(rr, zz, mm), device_id_type=pl.DeviceIdType.MESH)

    ld_wq = pltpu.make_async_copy(wq_h, wq_v, lsem.at[0])
    ld_x = pltpu.make_async_copy(x_h, x_v, lsem.at[1])
    ld_wk = pltpu.make_async_copy(wk_h, wk_v, lsem.at[2])
    ld_wv = pltpu.make_async_copy(wv_h, wv_v, lsem.at[3])
    ld_wo = pltpu.make_async_copy(wo_h, wo_v.at[m], lsem.at[4])
    ld_wq.start()
    ld_x.start()
    ld_wk.start()
    ld_wv.start()
    ld_wo.start()
    kcp, vcp = [], []
    for i in range(bl // CHUNK):
        src = pl.ds(start + i * CHUNK, CHUNK)
        dst = pl.ds(i * CHUNK, CHUNK)
        kcp.append(pltpu.make_async_copy(kc_h.at[src], k_v.at[dst], ksem.at[i]))
        vcp.append(pltpu.make_async_copy(vc_h.at[src], v_v.at[dst], vsem.at[i]))
    for i in range(bl // CHUNK):
        kcp[i].start()
        vcp[i].start()

    barrier = pltpu.get_barrier_semaphore()
    for k in range(1, 16):
        p = lax.rem(me + k, 16)
        pl.semaphore_signal(barrier, inc=1, device_id=(r, p // 4, p % 4),
                            device_id_type=pl.DeviceIdType.MESH)
    pl.semaphore_signal(barrier, inc=1, device_id=(1 - r, z, m),
                        device_id_type=pl.DeviceIdType.MESH)
    pl.semaphore_wait(barrier, 16)

    ld_wq.wait()
    ld_wq_rows = pl.ds(pl.multiple_of(r * hr, hr), hr)

    def a_half(tt, cd, i):
        zd = 2 * c + tt
        cols = pl.ds(tt * dh + cd * half, half)
        return rcopy(wq_v.at[ld_wq_rows, cols], wall.at[z, ld_wq_rows, :], a_s.at[i], a_r.at[z],
                     r, zd, yy * 2 + cd)

    def a_full(tt, cd, i):
        cols = pl.ds(tt * dh + cd * half, half)
        return rcopy(wq_v.at[:, cols], wall.at[z], a_s.at[i], a_r.at[z],
                     r, z, yy * 2 + cd)

    def a_self(tt, cd, i):
        cols = pl.ds(tt * dh + cd * half, half)
        return pltpu.make_async_copy(wq_v.at[:, cols], wall.at[z], a_s.at[i])

    def a_each(fn):
        for tt in range(2):
            for cd in range(2):
                i = tt * 2 + cd
                zd = 2 * c + tt

                @pl.when(zd != z)
                def _():
                    fn(a_half(tt, cd, i), False)

                @pl.when((zd == z) & (c != cd))
                def _():
                    fn(a_full(tt, cd, i), False)

                @pl.when((zd == z) & (c == cd))
                def _():
                    fn(a_self(tt, cd, i), True)

    a_each(lambda d, own: d.start())

    ld_wo.wait()
    wo_y = rcopy(wo_v.at[m], wo_v.at[m], w_s.at[0], w_r.at[0], r, z, mx)
    wo_d = rcopy(wo_v.at[m], wo_v.at[m], w_s.at[1], w_r.at[1], r, z, my)
    wo_y.start()
    wo_d.start()

    ld_x.wait()
    ld_wk.wait()
    kn_v[...] = jnp.dot(x_v[...], wk_v[...], preferred_element_type=F32).astype(BF)
    ld_wv.wait()
    vn_v[...] = jnp.dot(x_v[...], wv_v[...], preferred_element_type=F32).astype(BF)
    st_kn = pltpu.make_async_copy(kn_v, kn_h, osem.at[0])
    st_vn = pltpu.make_async_copy(vn_v, vn_h, osem.at[1])
    st_kn.start()
    st_vn.start()
    knf[...] = kn_v[pl.ds(start, bl), :].astype(F32)
    vnf[...] = vn_v[pl.ds(start, bl), :].astype(F32)

    ms = yy * 2 + z // 2

    def a_rec(zs):
        return rcopy(wall.at[zs, ld_wq_rows, :], wall.at[zs, ld_wq_rows, :], a_s.at[0], a_r.at[zs],
                     r, zs, ms)

    def x_fwd(zs):
        return rcopy(wall.at[zs, ld_wq_rows, :], wall.at[zs, ld_wq_rows, :], x_s.at[zs], x_r.at[zs],
                     1 - r, z, m)

    other = pl.ds(pl.multiple_of((1 - r) * hr, hr), hr)

    def x_rec(zs):
        return rcopy(wall.at[zs, other, :], wall.at[zs, other, :], x_s.at[zs], x_r.at[zs],
                     1 - r, z, m)

    def qdot(zs):
        cols = pl.ds(pl.multiple_of(zs * de, de), de)
        return jnp.dot(x_v[:, cols], wall[zs], preferred_element_type=F32)

    @pl.when(ms == m)
    def _():
        for tt in range(2):
            for cd in range(2):
                @pl.when((2 * c + tt == z) & (cd == c))
                def _():
                    a_self(tt, cd, tt * 2 + cd).wait()

    @pl.when(ms != m)
    def _():
        rcopy(wall.at[z], wall.at[z], a_s.at[0], a_r.at[z], r, z, my).wait_recv()

    qacc[...] = qdot(z)
    for k in range(1, 4):
        zs = lax.rem(z + k, 4)
        a_rec(zs).wait_recv()
        x_fwd(zs).start()
    for k in range(1, 4):
        zs = lax.rem(z + k, 4)
        x_rec(zs).wait_recv()
        qacc[...] += qdot(zs)
    q_my[...] = qacc[...].astype(BF).reshape(q_my.shape)

    slot = (4 * yy + z) * 2 + c
    for k in range(1, 16):
        p = lax.rem(me + k, 16)
        rcopy(q_my.at[p], q_in.at[slot], c_s.at[k - 1], c_r.at[slot], r, p // 4, p % 4).start()
    q_in[slot] = q_my[me]

    rcopy(wo_v.at[mx], wo_v.at[mx], w_s.at[0], w_r.at[0], r, z, mx).wait_recv()
    wo_f = rcopy(wo_v.at[mx], wo_v.at[mx], w_s.at[2], w_r.at[2], r, z, my)
    wo_f.start()

    for k in range(1, 16):
        s_ = lax.rem(slot + k, 16)
        rcopy(q_in.at[s_], q_in.at[s_], c_s.at[k - 1], c_r.at[s_], r, z, m).wait_recv()
    qf[...] = q_in[...].astype(F32).reshape(qf.shape)

    lane = lax.broadcasted_iota(jnp.int32, (nh, t), 1)

    def attend(base, bb):
        b = base + bb
        q = jnp.concatenate([qf[pl.ds(b, nh, stride=2 * bl), :],
                             qf[pl.ds(b + bl, nh, stride=2 * bl), :]], axis=1)
        s = lax.dot_general(q.astype(BF), k_v[b], (((1,), (1,)), ((), ())),
                            preferred_element_type=F32) * scale
        s = jnp.where(lane < lens[start + b], s, -jnp.inf)
        sn = jnp.sum(q * knf[pl.ds(b, 1), :], axis=1, keepdims=True) * scale
        mx_ = jnp.maximum(jnp.max(s, axis=1, keepdims=True), sn)
        p = jnp.exp(s - mx_)
        pn = jnp.exp(sn - mx_)
        l = jnp.sum(p, axis=1, keepdims=True) + pn
        acc = jnp.dot(p.astype(BF), v_v[b], preferred_element_type=F32)
        acc = acc + pn.astype(BF).astype(F32) * vnf[pl.ds(b, 1), :]
        return acc / l

    oz = pl.ds(pl.multiple_of(z * nb, nb), nb)

    def o_send(n, k):
        zd = lax.rem(z + k, 4)
        return rcopy(o_in.at[n, :, oz, :], o_in.at[n, :, oz, :], o_s.at[n, k - 1], o_r.at[n, z],
                     r, zd, m)

    def o_rec(n, zs):
        rows = pl.ds(pl.multiple_of(zs * nb, nb), nb)
        return rcopy(o_in.at[n, :, rows, :], o_in.at[n, :, rows, :], o_s.at[n, 0], o_r.at[n, zs],
                     r, zs, m)

    for n in range(NB):
        for i in range(nb // CHUNK):
            kcp[n * (nb // CHUNK) + i].wait()
            vcp[n * (nb // CHUNK) + i].wait()

        def group(g, carry):
            for u in range(UNROLL):
                bb = g * UNROLL + u
                o = attend(n * nb, bb)
                of[0, pl.ds(bb, nh, stride=nb), :] = o[:, :half]
                of[1, pl.ds(bb, nh, stride=nb), :] = o[:, half:]
            return carry

        lax.fori_loop(0, nb // UNROLL, group, 0)
        for h in range(nh):
            rows = slice(h * nb, (h + 1) * nb)
            o_in[n, h, oz, :] = jnp.concatenate([of[0, rows, :], of[1, rows, :]], axis=1).astype(BF)
        for k in range(1, 4):
            o_send(n, k).start()

    rcopy(wo_v.at[my], wo_v.at[my], w_s.at[1], w_r.at[1], r, z, my).wait_recv()
    md = (1 - yy) * 2 + 1 - c
    rcopy(wo_v.at[md], wo_v.at[md], w_s.at[2], w_r.at[2], r, z, my).wait_recv()

    def blk(n, zs, ms_):
        return y_v.at[:, ms_, pl.ds(n * nb, nb), pl.ds(pl.multiple_of(zs * de, de), de)]

    def yz_send(n, k):
        zd = lax.rem(z + k, 4)
        return rcopy(blk(n, z, m), blk(n, z, m), yz_s.at[n, k - 1], yz_r.at[n, z], r, zd, m)

    def yz_rec(n, zs):
        return rcopy(blk(n, zs, m), blk(n, zs, m), yz_s.at[n, 0], yz_r.at[n, zs], r, zs, m)

    def yy_send(n, zs):
        return rcopy(blk(n, zs, m), blk(n, zs, m), yy_s.at[n, zs], yy_r.at[n, zs], r, z, mx)

    def yy_rec(n, zs):
        return rcopy(blk(n, zs, mx), blk(n, zs, mx), yy_s.at[n, zs], yy_r.at[n, zs], r, z, mx)

    def yd_send(n, zs, hop):
        ms_ = mx if hop else m
        return rcopy(blk(n, zs, ms_), blk(n, zs, ms_), yd_s.at[n, hop, zs], yd_r.at[n, hop, zs],
                     r, z, my)

    def yd_rec(n, zs, hop):
        ms_ = md if hop else my
        return rcopy(blk(n, zs, ms_), blk(n, zs, ms_), yd_s.at[n, hop, zs], yd_r.at[n, hop, zs],
                     r, z, my)

    for n in range(NB):
        for k in range(1, 4):
            o_rec(n, lax.rem(z + k, 4)).wait_recv()
        acc = jnp.zeros((4 * nb, de), F32)
        for h in range(nh):
            acc = acc + jnp.dot(o_in[n, h], wo_v[h // 2, (h % 2) * dh:(h % 2 + 1) * dh, :],
                                preferred_element_type=F32)
        zc = pl.ds(pl.multiple_of(z * de, de), de)
        for zs in range(4):
            rows = pl.ds(pl.multiple_of(zs * 4 * bl + m * bl + n * nb, nb), nb)
            yb = x_v[rows, zc].astype(F32) + acc[zs * nb:(zs + 1) * nb]
            y_v[zs, m, n * nb:(n + 1) * nb, zc] = yb.astype(BF)
        for k in range(1, 4):
            yz_send(n, k).start()
        yy_send(n, z).start()
        yd_send(n, z, 0).start()

    for n in range(NB):
        for k in range(1, 4):
            zs = lax.rem(z + k, 4)
            yz_rec(n, zs).wait_recv()
            yy_send(n, zs).start()
            yd_send(n, zs, 0).start()
    for n in range(NB):
        for k in range(4):
            zs = lax.rem(z + k, 4)
            yy_rec(n, zs).wait_recv()
            yd_send(n, zs, 1).start()
    for n in range(NB):
        for hop in range(2):
            for k in range(4):
                yd_rec(n, lax.rem(z + k, 4), hop).wait_recv()

    st_y = pltpu.make_async_copy(y_v, y_h, osem.at[2])
    st_y.start()

    a_each(lambda d, own: None if own else d.wait_send())
    for k in range(1, 4):
        x_fwd(lax.rem(z + k, 4)).wait_send()
    for k in range(1, 16):
        p = lax.rem(me + k, 16)
        rcopy(q_my.at[p], q_in.at[slot], c_s.at[k - 1], c_r.at[slot], r, p // 4, p % 4).wait_send()
    wo_y.wait_send()
    wo_d.wait_send()
    wo_f.wait_send()
    for n in range(NB):
        for k in range(1, 4):
            o_send(n, k).wait_send()
            yz_send(n, k).wait_send()
        for zs in range(4):
            yy_send(n, zs).wait_send()
            yd_send(n, zs, 0).wait_send()
            yd_send(n, zs, 1).wait_send()
    st_kn.wait()
    st_vn.wait()
    st_y.wait()


def solution(mesh):
    ne = mesh.shape['emb']
    nm = mesh.shape['model']

    def local(x, Wq, Wk, Wv, Wo, Kc, Vc, lengths):
        b, d = x.shape
        t, dh = Kc.shape[1:]
        de = Wq.shape[0]
        bl = b // (ne * nm)
        nb = bl // NB
        nh = 8
        hbm = pl.BlockSpec(memory_space=pl.ANY)
        dma = pltpu.SemaphoreType.DMA
        y, kn, vn = pl.pallas_call(
            _kernel,
            out_shape=(jax.ShapeDtypeStruct((ne, nm, bl, d), BF),
                       jax.ShapeDtypeStruct((b, dh), BF),
                       jax.ShapeDtypeStruct((b, dh), BF)),
            in_specs=[hbm] * 7 + [pl.BlockSpec(memory_space=pltpu.SMEM)],
            out_specs=(hbm, hbm, hbm),
            scratch_shapes=[
                pltpu.VMEM((b, d), BF), pltpu.VMEM(Wq.shape, BF), pltpu.VMEM((ne, de, dh // 2), BF),
                pltpu.VMEM(Wk.shape, BF), pltpu.VMEM(Wv.shape, BF), pltpu.VMEM((nm,) + Wo.shape, BF),
                pltpu.VMEM((bl, t, dh), BF), pltpu.VMEM((bl, t, dh), BF),
                pltpu.VMEM((b, dh), BF), pltpu.VMEM((b, dh), BF),
                pltpu.VMEM((bl, dh), F32), pltpu.VMEM((bl, dh), F32),
                pltpu.VMEM((b, dh // 2), F32),
                pltpu.VMEM((16, bl, dh // 2), BF), pltpu.VMEM((16, bl, dh // 2), BF),
                pltpu.VMEM((16 * bl, dh // 2), F32),
                pltpu.VMEM((2, nh * nb, dh // 2), F32),
                pltpu.VMEM((NB, nh, ne * nb, dh), BF),
                pltpu.VMEM((ne, nm, bl, d), BF),
                dma((5,)), dma((bl // CHUNK,)), dma((bl // CHUNK,)), dma((3,)),
                dma((4,)), dma((4,)), dma((4,)), dma((4,)),
                dma((15,)), dma((16,)), dma((3,)), dma((3,)),
                dma((NB, 3)), dma((NB, 4)),
                dma((NB, 3)), dma((NB, 4)), dma((NB, 4)), dma((NB, 4)),
                dma((NB, 2, 4)), dma((NB, 2, 4)),
            ],
            compiler_params=pltpu.CompilerParams(
                collective_id=0, has_side_effects=True, vmem_limit_bytes=60 * 1024 * 1024),
        )(x, Wq, Wk, Wv, Wo, Kc, Vc, lengths)
        return y.reshape(b, d), kn, vn

    in_specs = (P('rep', None), P('emb', 'model'), P(), P(), P('model', 'emb'),
                P('rep', None, None), P('rep', None, None), P('rep'))
    out_specs = (P('rep', None), P('rep', None), P('rep', None))
    return jax.shard_map(local, mesh=mesh, in_specs=in_specs, out_specs=out_specs, check_vma=False)
```

time: 183 us -> 74.6 us (0.41)
  waiting for transfers between devices: 109 us -> 0 us
  Pallas kernels: 0 us -> 68 us
  matrix products: 24.7 us -> 0 us
  blocking collectives: 18.9 us -> 0 us
  between operations: 13.9 us -> 0.66 us
  starting transfers between devices: 4.91 us -> 0 us
  other arithmetic: 3.53 us -> 0 us
    pallas_call x0 -> x1, Pallas kernels: none -> 68 us  [local(): pl.pallas_call(_kernel, out_shape=(jax.ShapeDtypeStruct((ne, nm, bl, d),...]
    all_gather x1 -> x0, waiting for transfers between devices: 46.2 us -> none  [local(): y = lax.all_gather(yi, 'emb', axis=1, tiled=True)]
    psum x1 -> x0, waiting for transfers between devices: 33.8 us -> none  [local(): ys = lax.psum(yp, 'model')]
    reduce_scatter x1 -> x0, waiting for transfers between devices: 26.2 us -> none  [local(): q = lax.psum_scatter(qp, 'emb', scatter_dimension=0, tiled=True)]
    dot_general x7 -> x0, matrix products: 24.7 us -> none  [the longest x1 10.3 us: _attend(): jnp.einsum('bhd,btd->bht', q, K, preferred_element_type=jnp.float32) * scale]
    all_gather x1 -> x0, blocking collectives: 11.8 us -> none  [local(): o = lax.all_gather(o, 'emb', axis=0, tiled=True)]
    all_to_all x1 -> x0, blocking collectives: 7.12 us -> none  [local(): o = lax.all_to_all(o, 'model', 1, 0, tiled=True)]
    all_to_all x1 -> x0, starting transfers between devices: 4.82 us -> none  [local(): q = lax.all_to_all(q, 'model', 0, 1, tiled=True)]
  transfers between devices with their start and end apart: 4 -> 0, of which waited for: 4 -> 0; matrix products, arithmetic and copies ran while one was open for 2% -> 0% of each run, Pallas kernels for 0% -> 0%
where the time goes in v1:
time: 74.6 us; the launch traced here: 73.2 us
  Pallas kernels  68 us (91%)
  local copies, waits for them, and re-layouts  4.63 us (6%)
    pallas_call x1, Pallas kernels, local(): pl.pallas_call(_kernel, out_shape=(jax.ShapeDtypeStruct((ne, nm, bl, d),...  68 us
    unnamed x7, local copies, waits for them, and re-layouts  4.63 us

profile of v1, /device:TPU:1, one launch (start us, length us, event | category | flops | bytes accessed | tf_op | source)
XLA Modules:
  0.0 73.2 jit_solution(16153811082084229294)
XLA Ops:
  0.6 68.0 %shard_map.103 = (bf16[4,4,32,2048]{3,2,1,0:T(8,128)(2,1)}, bf16[512,256]{1,0:T(8,128)(2,1)}, bf16[512,256]{1,0:T(8,128)(2,1)}) custom-call(bf16[512,2048]{1,0:T(8,128)(2,1)} %x_h.1, bf16[512,512]{1,0:T(8,128)(2,1)} %wq_h.1, bf16[2048,256]{1,0:T(8,128)(2,1)} %wk_h.1, bf16[2048,256]{1,0:T(8,128)(2,1)} %wv_h.1, bf16[512,512]{1,0:T(8,128)(2,1)} %wo_h.1, ...), custom_call_target="tpu_custom_call" | custom-call | tf_op jit(solution)/shard_map/pallas_call | solution.py:342
  68.6 0.0 copy-start.1
  68.6 0.0 copy-start
  68.6 3.2 %copy.14 = bf16[512,2048]{1,0:T(8,128)(2,1)} copy(bf16[512,2048]{1,0:T(8,128)(2,1)} %bitcast.1) | data formatting | bytes 4194304
  71.8 0.0 copy-done.1
  71.8 0.7 copy.15
  72.5 0.0 copy-done
  72.5 0.7 copy.16
Async XLA Ops:
  68.6 3.2 %copy-start.1 = (bf16[512,256]{1,0:T(8,128)(2,1)S(1)}, bf16[512,256]{1,0:T(8,128)(2,1)}, u32[]{:S(2)}) copy-start(bf16[512,256]{1,0:T(8,128)(2,1)} %get-tuple-element.13) | copy-start | bytes 786436
  68.6 3.9 %copy-start = (bf16[512,256]{1,0:T(8,128)(2,1)S(1)}, bf16[512,256]{1,0:T(8,128)(2,1)}, u32[]{:S(2)}) copy-start(bf16[512,256]{1,0:T(8,128)(2,1)} %get-tuple-element.14) | copy-start | bytes 786436

commit v2 on v1

v2 whole, which is shorter than its diff:
```python
import functools

import jax
import jax.numpy as jnp
from jax import lax
from jax.experimental import pallas as pl
from jax.experimental.pallas import tpu as pltpu
from jax.sharding import PartitionSpec as P

BF = jnp.bfloat16
F32 = jnp.float32
NB = 4
J0 = 160
LAG = 2
VMEM_LIMIT = 54 * 1024 * 1024
CHUNK = 8


def _kernel(x_h, wq_h, wk_h, wv_h, wo_h, kc_h, vc_h, lens,
            y_v, kn_v, vn_v,
            x_v, wq_v, wall, wk_v, wv_v, wst, wo_v, k_v, v_v, knf, vnf,
            qacc, q_my, q_in, qf, of, o_in,
            lsem, ksem, vsem,
            a_s, a_r, x_s, x_r, c_s, c_r, w1_s, w1_r, w2_s, w3_s, wn_s, wt_s, wn_r, wt_r,
            o_s, o_r, yz_s, yz_r, yy_s, yy_r, yd_s, yd_r):
    r = lax.axis_index('rep')
    z = lax.axis_index('emb')
    m = lax.axis_index('model')
    yy = m // 2
    c = m % 2
    my = yy * 2 + 1 - c
    mx = (1 - yy) * 2 + c
    near = z + 1 - 2 * (z % 2)
    z2 = lax.rem(z + 2, 4)
    me = z * 4 + m
    bl = k_v.shape[0]
    nb = bl // NB
    t = k_v.shape[1]
    dh = k_v.shape[2]
    nh = 8
    half = dh // 2
    de = wq_v.shape[0]
    hr = de // 2
    start = pl.multiple_of(me * bl, bl)
    scale = dh ** -0.5

    def rcopy(src, dst, ss, rs, rr, zz, mm):
        return pltpu.make_async_remote_copy(
            src_ref=src, dst_ref=dst, send_sem=ss, recv_sem=rs,
            device_id=(rr, zz, mm), device_id_type=pl.DeviceIdType.MESH)

    ld_wq = pltpu.make_async_copy(wq_h, wq_v, lsem.at[0])
    ld_x = pltpu.make_async_copy(x_h, x_v, lsem.at[1])
    ld_wk = pltpu.make_async_copy(wk_h, wk_v, lsem.at[2])
    ld_wv = pltpu.make_async_copy(wv_h, wv_v, lsem.at[3])
    ld_wo = pltpu.make_async_copy(wo_h, wst, lsem.at[4])
    ld_wq.start()
    ld_x.start()
    ld_wk.start()
    ld_wv.start()
    ld_wo.start()
    kcp, vcp = [], []
    for i in range(bl // CHUNK):
        src = pl.ds(start + i * CHUNK, CHUNK)
        dst = pl.ds(i * CHUNK, CHUNK)
        kcp.append(pltpu.make_async_copy(kc_h.at[src], k_v.at[dst], ksem.at[i]))
        vcp.append(pltpu.make_async_copy(vc_h.at[src], v_v.at[dst], vsem.at[i]))

    barrier = pltpu.get_barrier_semaphore()
    for k in range(1, 16):
        p = lax.rem(me + k, 16)
        pl.semaphore_signal(barrier, inc=1, device_id=(r, p // 4, p % 4),
                            device_id_type=pl.DeviceIdType.MESH)
    pl.semaphore_signal(barrier, inc=1, device_id=(1 - r, z, m),
                        device_id_type=pl.DeviceIdType.MESH)
    pl.semaphore_wait(barrier, 16)

    ld_wq.wait()
    ld_wq_rows = pl.ds(pl.multiple_of(r * hr, hr), hr)

    def a_half(tt, cd, i):
        zd = 2 * c + tt
        cols = pl.ds(tt * dh + cd * half, half)
        return rcopy(wq_v.at[ld_wq_rows, cols], wall.at[z, ld_wq_rows, :], a_s.at[i], a_r.at[z],
                     r, zd, yy * 2 + cd)

    def a_full(tt, cd, i):
        cols = pl.ds(tt * dh + cd * half, half)
        return rcopy(wq_v.at[:, cols], wall.at[z], a_s.at[i], a_r.at[z],
                     r, z, yy * 2 + cd)

    def a_self(tt, cd, i):
        cols = pl.ds(tt * dh + cd * half, half)
        return pltpu.make_async_copy(wq_v.at[:, cols], wall.at[z], a_s.at[i])

    def a_each(fn):
        for first in range(2):
            @pl.when(z % 2 == first)
            def _():
                for tt in (first, 1 - first):
                    for cd in range(2):
                        i = tt * 2 + cd
                        zd = 2 * c + tt

                        @pl.when(zd != z)
                        def _():
                            fn(a_half(tt, cd, i), False)

                        @pl.when((zd == z) & (c != cd))
                        def _():
                            fn(a_full(tt, cd, i), False)

                        @pl.when((zd == z) & (c == cd))
                        def _():
                            fn(a_self(tt, cd, i), True)

    a_each(lambda d, own: d.start())

    far = c != z // 2
    ld_wo.wait()
    w_own = pltpu.make_async_copy(wst, wo_v.at[m], lsem.at[5])
    w_d2d = rcopy(wst, wo_v.at[m], w1_s.at[0], w1_r.at[0], r, z, my)

    def w_y(i):
        rows = pl.ds(i * hr, hr)
        return rcopy(wst.at[rows, :], wo_v.at[m, rows, :], w2_s.at[i], wn_r.at[m, i],
                     r, z, (1 - yy) * 2 + z // 2)

    def w_rows(g, j):
        return pl.ds(pl.multiple_of(g * hr + j * J0, 16), hr - J0 if j else J0)

    def w_z(j):
        return rcopy(wst.at[w_rows(r, j), :], wo_v.at[m, w_rows(r, j), :], w3_s.at[j], wn_r.at[m, j],
                     r, z2, yy * 2 + z // 2)

    def w_half(mm, j):
        return wo_v.at[mm, w_rows(r, j), :]

    def w_next(k, j):
        mm = 2 * yy + k
        return rcopy(w_half(mm, j), w_half(mm, j), wn_s.at[k, j], wn_r.at[mm, j], r, z, mx)

    def w_twin(mm, j):
        return rcopy(w_half(mm, j), w_half(mm, j), wt_s.at[mm, j], wt_r.at[mm, j], 1 - r, z, m)

    def w_arrived(mm, j):
        return rcopy(w_half(mm, j), w_half(mm, j), wt_s.at[mm, j], wn_r.at[mm, j], r, z, mx)

    def w_pass_z(j):
        @pl.when(far)
        def _():
            for k in range(2):
                w_arrived(2 * yy + k, j).wait_recv()
                w_next(k, j).start()
                w_twin(2 * yy + k, j).start()

    def w_pass_y(j):
        @pl.when(far)
        def _():
            for k in range(2):
                w_arrived(2 * (1 - yy) + k, j).wait_recv()
                w_twin(2 * (1 - yy) + k, j).start()

    def w_wait():
        @pl.when(far)
        def _():
            for mm in range(4):
                for j in range(2):
                    part = wo_v.at[mm, w_rows(1 - r, j), :]
                    rcopy(part, part, wt_s.at[mm, j], wt_r.at[mm, j], 1 - r, z, m).wait_recv()

        @pl.when(~far)
        def _():
            w_own.wait()
            rcopy(wst, wo_v.at[my], w1_s.at[0], w1_r.at[0], r, z, my).wait_recv()
            for k in range(2):
                for i in range(2):
                    part = wo_v.at[2 * (1 - yy) + k, pl.ds(i * hr, hr), :]
                    rcopy(part, part, w2_s.at[i], wn_r.at[2 * (1 - yy) + k, i], r, z, mx).wait_recv()

    @pl.when(far)
    def _():
        w_d2d.start()

    @pl.when(~far)
    def _():
        w_own.start()

    w_z(0).start()
    w_y(0).start()

    ld_x.wait()
    ld_wk.wait()
    ld_wv.wait()
    for i in range(bl // CHUNK):
        kcp[i].start()
        vcp[i].start()
    kn_v[...] = jnp.dot(x_v[...], wk_v[...], preferred_element_type=F32).astype(BF)
    vn_v[...] = jnp.dot(x_v[...], wv_v[...], preferred_element_type=F32).astype(BF)
    knf[...] = kn_v[pl.ds(start, bl), :].astype(F32)
    vnf[...] = vn_v[pl.ds(start, bl), :].astype(F32)

    ms = yy * 2 + z // 2

    def a_rec(zs):
        return rcopy(wall.at[zs, ld_wq_rows, :], wall.at[zs, ld_wq_rows, :], a_s.at[0], a_r.at[zs],
                     r, zs, ms)

    def x_fwd(zs):
        return rcopy(wall.at[zs, ld_wq_rows, :], wall.at[zs, ld_wq_rows, :], x_s.at[zs], x_r.at[zs],
                     1 - r, z, m)

    other = pl.ds(pl.multiple_of((1 - r) * hr, hr), hr)

    def x_rec(zs):
        return rcopy(wall.at[zs, other, :], wall.at[zs, other, :], x_s.at[zs], x_r.at[zs],
                     1 - r, z, m)

    def qdot(zs):
        cols = pl.ds(pl.multiple_of(zs * de, de), de)
        return jnp.dot(x_v[:, cols], wall[zs], preferred_element_type=F32)

    @pl.when(ms == m)
    def _():
        for tt in range(2):
            for cd in range(2):
                @pl.when((2 * c + tt == z) & (cd == c))
                def _():
                    a_self(tt, cd, tt * 2 + cd).wait()

    @pl.when(ms != m)
    def _():
        rcopy(wall.at[z], wall.at[z], a_s.at[0], a_r.at[z], r, z, my).wait_recv()

    qacc[...] = qdot(z)
    for zs in (near, z2, 3 - z):
        a_rec(zs).wait_recv()
        x_fwd(zs).start()
    for zs in (near, z2, 3 - z):
        x_rec(zs).wait_recv()
        qacc[...] += qdot(zs)
    q_my[...] = qacc[...].astype(BF).reshape(q_my.shape)

    slot = (4 * yy + z) * 2 + c
    for k in range(1, 16):
        p = lax.rem(me + k, 16)
        rcopy(q_my.at[p], q_in.at[slot], c_s.at[k - 1], c_r.at[slot], r, p // 4, p % 4).start()
    q_in[slot] = q_my[me]

    w_z(1).start()
    w_y(1).start()
    w_pass_z(0)

    for k in range(1, 16):
        s_ = lax.rem(slot + k, 16)
        rcopy(q_in.at[s_], q_in.at[s_], c_s.at[k - 1], c_r.at[s_], r, z, m).wait_recv()
    qf[...] = q_in[...].astype(F32).reshape(qf.shape)

    lane = lax.broadcasted_iota(jnp.int32, (nh, t), 1)

    def query(b):
        return jnp.concatenate([qf[pl.ds(b, nh, stride=2 * bl), :],
                                qf[pl.ds(b + bl, nh, stride=2 * bl), :]], axis=1)

    def scores(b):
        return lax.dot_general(query(b).astype(BF), k_v[b], (((1,), (1,)), ((), ())),
                               preferred_element_type=F32) * scale

    def weights(b, s):
        s = jnp.where(lane < lens[start + b], s, -jnp.inf)
        sn = jnp.sum(query(b) * knf[pl.ds(b, 1), :], axis=1, keepdims=True) * scale
        top = jnp.maximum(jnp.max(s, axis=1, keepdims=True), sn)
        p = jnp.exp(s - top)
        pn = jnp.exp(sn - top)
        return p.astype(BF), pn, jnp.sum(p, axis=1, keepdims=True) + pn

    def values(b, bb, p, pn, l):
        acc = jnp.dot(p, v_v[b], preferred_element_type=F32)
        o = (acc + pn.astype(BF).astype(F32) * vnf[pl.ds(b, 1), :]) / l
        of[0, pl.ds(bb, nh, stride=nb), :] = o[:, :half]
        of[1, pl.ds(bb, nh, stride=nb), :] = o[:, half:]

    def attend(base):
        s, p = {}, {}
        for i in range(nb + 2 * LAG):
            if i < nb:
                s[i] = scores(base + i)
            if LAG <= i < nb + LAG:
                p[i - LAG] = weights(base + i - LAG, s.pop(i - LAG))
            if i >= 2 * LAG:
                values(base + i - 2 * LAG, i - 2 * LAG, *p.pop(i - 2 * LAG))

    pair = 2 * (z // 2)
    pos = z % 2
    og = pos * 2 + c

    def o_send(n, k):
        return rcopy(o_in.at[n, og], o_in.at[n, og], o_s.at[n, k], o_r.at[n, og],
                     r, z if k == 0 else near, my if k == 0 else m)

    ng = (1 - pos) * 2 + c

    def o_pass(n):
        return rcopy(o_in.at[n, ng], o_in.at[n, ng], o_s.at[n, 2], o_r.at[n, ng], r, z, my)

    def o_rec(n, g):
        return rcopy(o_in.at[n, g], o_in.at[n, g], o_s.at[n, 0], o_r.at[n, g], r, near, m)

    def o_mid(n):
        o_rec(n, ng).wait_recv()
        o_pass(n).start()

    def blk(n, zs, ms_):
        cols = pl.ds(pl.multiple_of((zs % 2 + 2 * (ms_ % 2)) * de, de), de)
        return y_v.at[pl.ds(2 * (zs // 2), 2), pl.ds(2 * (ms_ // 2), 2), pl.ds(n * nb, nb), cols]

    others = (near, z2, 3 - z)

    def yz_send(n, k):
        return rcopy(blk(n, z, m), blk(n, z, m), yz_s.at[n, k], yz_r.at[n, z], r, others[k], m)

    def yz_rec(n, zs):
        return rcopy(blk(n, zs, m), blk(n, zs, m), yz_s.at[n, 0], yz_r.at[n, zs], r, near, m)

    def yy_send(n, zs):
        return rcopy(blk(n, zs, m), blk(n, zs, m), yy_s.at[n, zs], yy_r.at[n, zs], r, z, mx)

    def yy_rec(n, zs):
        return rcopy(blk(n, zs, mx), blk(n, zs, mx), yy_s.at[n, zs], yy_r.at[n, zs], r, z, mx)

    md = (1 - yy) * 2 + 1 - c

    def yd_send(n, zs, hop):
        ms_ = mx if hop else m
        return rcopy(blk(n, zs, ms_), blk(n, zs, ms_), yd_s.at[n, hop, zs], yd_r.at[n, hop, zs],
                     r, z, my)

    def yd_rec(n, zs, hop):
        ms_ = md if hop else my
        return rcopy(blk(n, zs, ms_), blk(n, zs, ms_), yd_s.at[n, hop, zs], yd_r.at[n, hop, zs],
                     r, z, my)

    def project(n):
        o_rec(n, pos * 2 + 1 - c).wait_recv()
        o_rec(n, (1 - pos) * 2 + 1 - c).wait_recv()
        ob = [o_in[n, g].astype(F32) for g in range(4)]
        acc = jnp.zeros((4 * nb, de), F32)
        for h in range(nh):
            lhs = jnp.concatenate([ob[g][h * nb:(h + 1) * nb] for g in range(4)], axis=0).astype(BF)
            acc = acc + jnp.dot(lhs, wo_v[h // 2, (h % 2) * dh:(h % 2 + 1) * dh, :],
                                preferred_element_type=F32)
        cols = pl.ds(pl.multiple_of((z % 2 + 2 * c) * de, de), de)
        for g in range(4):
            zz = pair + g // 2
            mm = 2 * yy + g % 2
            xr = x_v[pl.ds(pl.multiple_of((zz * 4 + mm) * bl, bl), bl), cols].astype(F32)
            yb = xr[n * nb:(n + 1) * nb] + acc[g * nb:(g + 1) * nb]
            y_v[zz, mm, n * nb:(n + 1) * nb, cols] = yb.astype(BF)
        for k in (2, 1, 0):
            yz_send(n, k).start()
        yy_send(n, z).start()
        yd_send(n, z, 0).start()

    def drain_z(n):
        for zs in others:
            yz_rec(n, zs).wait_recv()
            yy_send(n, zs).start()
            yd_send(n, zs, 0).start()

    def drain_y(n):
        for zs in (z,) + others:
            yy_rec(n, zs).wait_recv()
            yd_send(n, zs, 1).start()

    for n in range(NB):
        for i in range(n * nb // CHUNK, (n + 1) * nb // CHUNK):
            kcp[i].wait()
            vcp[i].wait()
        attend(n * nb)
        o_in[n, og] = jnp.concatenate([of[0], of[1]], axis=1).astype(BF)
        o_send(n, 1).start()
        o_send(n, 0).start()
        if n == 0:
            w_pass_y(0)
            w_pass_z(1)
        else:
            o_mid(n - 1)
        if n == 2:
            w_pass_y(1)

    w_wait()
    for n in range(NB - 1):
        project(n)
    o_mid(NB - 1)
    drain_z(0)
    project(NB - 1)
    for n in range(1, NB):
        drain_z(n)
        drain_y(n - 1)
    drain_y(NB - 1)
    for n in range(NB):
        for hop in range(2):
            for zs in range(4):
                yd_rec(n, zs, hop).wait_recv()

    a_each(lambda d, own: None if own else d.wait_send())
    for k in range(1, 4):
        x_fwd(lax.rem(z + k, 4)).wait_send()
    for k in range(1, 16):
        p = lax.rem(me + k, 16)
        rcopy(q_my.at[p], q_in.at[slot], c_s.at[k - 1], c_r.at[slot], r, p // 4, p % 4).wait_send()
    @pl.when(far)
    def _():
        w_d2d.wait_send()
        for j in range(2):
            for k in range(2):
                w_next(k, j).wait_send()
            for mm in range(4):
                w_twin(mm, j).wait_send()

    for i in range(2):
        w_y(i).wait_send()
        w_z(i).wait_send()
    for n in range(NB):
        for k in range(2):
            o_send(n, k).wait_send()
        o_pass(n).wait_send()
        for k in range(3):
            yz_send(n, k).wait_send()
        for zs in range(4):
            yy_send(n, zs).wait_send()
            yd_send(n, zs, 0).wait_send()
            yd_send(n, zs, 1).wait_send()


def solution(mesh):
    ne = mesh.shape['emb']
    nm = mesh.shape['model']

    def local(x, Wq, Wk, Wv, Wo, Kc, Vc, lengths):
        b, d = x.shape
        t, dh = Kc.shape[1:]
        de = Wq.shape[0]
        bl = b // (ne * nm)
        nb = bl // NB
        nh = 8
        hbm = pl.BlockSpec(memory_space=pl.ANY)
        vmem = pl.BlockSpec(memory_space=pltpu.VMEM)
        dma = pltpu.SemaphoreType.DMA
        y, kn, vn = pl.pallas_call(
            _kernel,
            out_shape=(pltpu.VMEM((ne, nm, bl, d), BF), pltpu.VMEM((b, dh), BF),
                       pltpu.VMEM((b, dh), BF)),
            in_specs=[hbm] * 7 + [pl.BlockSpec(memory_space=pltpu.SMEM)],
            out_specs=(vmem, vmem, vmem),
            scratch_shapes=[
                pltpu.VMEM((b, d), BF), pltpu.VMEM(Wq.shape, BF), pltpu.VMEM((ne, de, dh // 2), BF),
                pltpu.VMEM(Wk.shape, BF), pltpu.VMEM(Wv.shape, BF), pltpu.VMEM(Wo.shape, BF),
                pltpu.VMEM((nm,) + Wo.shape, BF),
                pltpu.VMEM((bl, t, dh), BF), pltpu.VMEM((bl, t, dh), BF),
                pltpu.VMEM((bl, dh), F32), pltpu.VMEM((bl, dh), F32),
                pltpu.VMEM((b, dh // 2), F32),
                pltpu.VMEM((16, bl, dh // 2), BF), pltpu.VMEM((16, bl, dh // 2), BF),
                pltpu.VMEM((16 * bl, dh // 2), F32),
                pltpu.VMEM((2, nh * nb, dh // 2), F32),
                pltpu.VMEM((NB, 4, nh * nb, dh), BF),
                dma((6,)), dma((bl // CHUNK,)), dma((bl // CHUNK,)),
                dma((4,)), dma((4,)), dma((4,)), dma((4,)), dma((15,)), dma((16,)),
                dma((1,)), dma((1,)), dma((2,)), dma((2,)), dma((2, 2)), dma((4, 2)),
                dma((4, 2)), dma((4, 2)),
                dma((NB, 3)), dma((NB, 4)), dma((NB, 3)), dma((NB, 4)),
                dma((NB, 4)), dma((NB, 4)), dma((NB, 2, 4)), dma((NB, 2, 4)),
            ],
            compiler_params=pltpu.CompilerParams(
                collective_id=0, has_side_effects=True, vmem_limit_bytes=VMEM_LIMIT),
        )(x, Wq, Wk, Wv, Wo, Kc, Vc, lengths)
        return y.reshape(b, d), kn, vn

    in_specs = (P('rep', None), P('emb', 'model'), P(), P(), P('model', 'emb'),
                P('rep', None, None), P('rep', None, None), P('rep'))
    out_specs = (P('rep', None), P('rep', None), P('rep', None))
    return jax.shard_map(local, mesh=mesh, in_specs=in_specs, out_specs=out_specs, check_vma=False)
```

time: 74.6 us -> 66.5 us (0.89); the launches traced: 73.2 us -> 66.4 us
  Pallas kernels: 68 us -> 63 us
  local copies, waits for them, and re-layouts: 4.63 us -> 2.73 us
    pallas_call x1, Pallas kernels: 68 us -> 63 us  [local(): pl.pallas_call(_kernel, out_shape=(pltpu.VMEM((ne, nm, bl, d), BF), pltpu...]
    unnamed x7 -> x3, local copies, waits for them, and re-layouts: 4.63 us -> 2.73 us
where the time goes in v2:
time: 66.5 us; the launch traced here: 66.4 us
  Pallas kernels  63 us (95%)
  local copies, waits for them, and re-layouts  2.73 us (4%)
    pallas_call x1, Pallas kernels, local(): pl.pallas_call(_kernel, out_shape=(pltpu.VMEM((ne, nm, bl, d), BF), pltpu...  63 us
    unnamed x3, local copies, waits for them, and re-layouts  2.73 us

profile of v2, /device:TPU:1, one launch (start us, length us, event | category | flops | bytes accessed | tf_op | source)
XLA Modules:
  0.0 66.4 jit_solution(7012596967814796856)
XLA Ops:
  0.6 63.0 %shard_map.103 = (bf16[4,4,32,2048]{3,2,1,0:T(8,128)(2,1)S(1)}, bf16[512,256]{1,0:T(8,128)(2,1)S(1)}, bf16[512,256]{1,0:T(8,128)(2,1)S(1)}) custom-call(bf16[512,2048]{1,0:T(8,128)(2,1)} %x_h.1, bf16[512,512]{1,0:T(8,128)(2,1)} %wq_h.1, bf16[2048,256]{1,0:T(8,128)(2,1)} %wk_h.1, bf16[2048,256]{1,0:T(8,128)(2,1)} %wv_h.1, bf16[512,512]{1,0:T(8,128)(2,1)} %wo_h.1, ...), custom_call_target="tpu_custom_call" | custom-call | tf_op jit(solution)/shard_map/pallas_call | solution.py:450
  63.6 1.3 %copy.14 = bf16[512,2048]{1,0:T(8,128)(2,1)} copy(bf16[512,2048]{1,0:T(8,128)(2,1)S(1)} %bitcast.1) | data formatting | bytes 4194304
  64.9 0.7 %copy.15 = bf16[512,256]{1,0:T(8,128)(2,1)} copy(bf16[512,256]{1,0:T(8,128)(2,1)S(1)} %get-tuple-element.10) | data formatting | bytes 524288
  65.7 0.7 %copy.16 = bf16[512,256]{1,0:T(8,128)(2,1)} copy(bf16[512,256]{1,0:T(8,128)(2,1)S(1)} %get-tuple-element.11) | data formatting | bytes 524288

commit v3 on v2

--- a/solution.py
+++ b/solution.py
@@ -10,7 +10,7 @@
 BF = jnp.bfloat16
 F32 = jnp.float32
 NB = 4
-J0 = 160
+J0 = 96
 LAG = 2
 VMEM_LIMIT = 54 * 1024 * 1024
 CHUNK = 8
@@ -116,7 +116,7 @@
 
     a_each(lambda d, own: d.start())
 
-    far = c != z // 2
+    far = c != z % 2
     ld_wo.wait()
     w_own = pltpu.make_async_copy(wst, wo_v.at[m], lsem.at[5])
     w_d2d = rcopy(wst, wo_v.at[m], w1_s.at[0], w1_r.at[0], r, z, my)
@@ -124,14 +124,14 @@
     def w_y(i):
         rows = pl.ds(i * hr, hr)
         return rcopy(wst.at[rows, :], wo_v.at[m, rows, :], w2_s.at[i], wn_r.at[m, i],
-                     r, z, (1 - yy) * 2 + z // 2)
+                     r, z, (1 - yy) * 2 + z % 2)
 
     def w_rows(g, j):
         return pl.ds(pl.multiple_of(g * hr + j * J0, 16), hr - J0 if j else J0)
 
     def w_z(j):
         return rcopy(wst.at[w_rows(r, j), :], wo_v.at[m, w_rows(r, j), :], w3_s.at[j], wn_r.at[m, j],
-                     r, z2, yy * 2 + z // 2)
+                     r, near, yy * 2 + z % 2)
 
     def w_half(mm, j):
         return wo_v.at[mm, w_rows(r, j), :]
@@ -236,6 +236,7 @@
     for zs in (near, z2, 3 - z):
         a_rec(zs).wait_recv()
         x_fwd(zs).start()
+    w_z(1).start()
     for zs in (near, z2, 3 - z):
         x_rec(zs).wait_recv()
         qacc[...] += qdot(zs)
@@ -247,9 +248,9 @@
         rcopy(q_my.at[p], q_in.at[slot], c_s.at[k - 1], c_r.at[slot], r, p // 4, p % 4).start()
     q_in[slot] = q_my[me]
 
-    w_z(1).start()
+    w_pass_z(0)
+    w_pass_z(1)
     w_y(1).start()
-    w_pass_z(0)
 
     for k in range(1, 16):
         s_ = lax.rem(slot + k, 16)
@@ -290,13 +291,12 @@
             if i >= 2 * LAG:
                 values(base + i - 2 * LAG, i - 2 * LAG, *p.pop(i - 2 * LAG))
 
-    pair = 2 * (z // 2)
-    pos = z % 2
+    pos = z // 2
     og = pos * 2 + c
 
     def o_send(n, k):
         return rcopy(o_in.at[n, og], o_in.at[n, og], o_s.at[n, k], o_r.at[n, og],
-                     r, z if k == 0 else near, my if k == 0 else m)
+                     r, z if k == 0 else z2, my if k == 0 else m)
 
     ng = (1 - pos) * 2 + c
 
@@ -304,17 +304,17 @@
         return rcopy(o_in.at[n, ng], o_in.at[n, ng], o_s.at[n, 2], o_r.at[n, ng], r, z, my)
 
     def o_rec(n, g):
-        return rcopy(o_in.at[n, g], o_in.at[n, g], o_s.at[n, 0], o_r.at[n, g], r, near, m)
+        return rcopy(o_in.at[n, g], o_in.at[n, g], o_s.at[n, 0], o_r.at[n, g], r, z2, m)
 
     def o_mid(n):
         o_rec(n, ng).wait_recv()
         o_pass(n).start()
 
     def blk(n, zs, ms_):
-        cols = pl.ds(pl.multiple_of((zs % 2 + 2 * (ms_ % 2)) * de, de), de)
-        return y_v.at[pl.ds(2 * (zs // 2), 2), pl.ds(2 * (ms_ // 2), 2), pl.ds(n * nb, nb), cols]
-
-    others = (near, z2, 3 - z)
+        cols = pl.ds(pl.multiple_of((2 * (zs // 2) + ms_ % 2) * de, de), de)
+        return y_v.at[:, zs % 2, pl.ds(2 * (ms_ // 2), 2), pl.ds(n * nb, nb), cols]
+
+    others = (near, 2 - z // 2, 3 - 3 * (z // 2))
 
     def yz_send(n, k):
         return rcopy(blk(n, z, m), blk(n, z, m), yz_s.at[n, k], yz_r.at[n, z], r, others[k], m)
@@ -349,23 +349,26 @@
             lhs = jnp.concatenate([ob[g][h * nb:(h + 1) * nb] for g in range(4)], axis=0).astype(BF)
             acc = acc + jnp.dot(lhs, wo_v[h // 2, (h % 2) * dh:(h % 2 + 1) * dh, :],
                                 preferred_element_type=F32)
-        cols = pl.ds(pl.multiple_of((z % 2 + 2 * c) * de, de), de)
+        cols = pl.ds(pl.multiple_of((2 * (z // 2) + c) * de, de), de)
         for g in range(4):
-            zz = pair + g // 2
             mm = 2 * yy + g % 2
-            xr = x_v[pl.ds(pl.multiple_of((zz * 4 + mm) * bl, bl), bl), cols].astype(F32)
+            row = ((z % 2 + 2 * (g // 2)) * 4 + mm) * bl
+            xr = x_v[pl.ds(pl.multiple_of(row, bl), bl), cols].astype(F32)
             yb = xr[n * nb:(n + 1) * nb] + acc[g * nb:(g + 1) * nb]
-            y_v[zz, mm, n * nb:(n + 1) * nb, cols] = yb.astype(BF)
+            y_v[g // 2, z % 2, mm, n * nb:(n + 1) * nb, cols] = yb.astype(BF)
         for k in (2, 1, 0):
             yz_send(n, k).start()
         yy_send(n, z).start()
         yd_send(n, z, 0).start()
 
+    def spread(n, zs):
+        yy_send(n, zs).start()
+        yd_send(n, zs, 0).start()
+
     def drain_z(n):
         for zs in others:
             yz_rec(n, zs).wait_recv()
-            yy_send(n, zs).start()
-            yd_send(n, zs, 0).start()
+            spread(n, zs)
 
     def drain_y(n):
         for zs in (z,) + others:
@@ -380,24 +383,26 @@
         o_in[n, og] = jnp.concatenate([of[0], of[1]], axis=1).astype(BF)
         o_send(n, 1).start()
         o_send(n, 0).start()
-        if n == 0:
-            w_pass_y(0)
-            w_pass_z(1)
-        else:
-            o_mid(n - 1)
-        if n == 2:
-            w_pass_y(1)
+        if n > 1:
+            o_mid(n - 2)
+        if n < 2:
+            w_pass_y(n)
 
     w_wait()
-    for n in range(NB - 1):
-        project(n)
-    o_mid(NB - 1)
+    project(0)
+    project(1)
+    o_mid(2)
+    project(2)
+    o_mid(3)
+    project(3)
     drain_z(0)
-    project(NB - 1)
-    for n in range(1, NB):
-        drain_z(n)
-        drain_y(n - 1)
-    drain_y(NB - 1)
+    drain_z(1)
+    drain_y(0)
+    drain_z(2)
+    drain_y(1)
+    drain_z(3)
+    drain_y(2)
+    drain_y(3)
     for n in range(NB):
         for hop in range(2):
             for zs in range(4):
@@ -449,7 +454,7 @@
         dma = pltpu.SemaphoreType.DMA
         y, kn, vn = pl.pallas_call(
             _kernel,
-            out_shape=(pltpu.VMEM((ne, nm, bl, d), BF), pltpu.VMEM((b, dh), BF),
+            out_shape=(pltpu.VMEM((2, ne // 2, nm, bl, d), BF), pltpu.VMEM((b, dh), BF),
                        pltpu.VMEM((b, dh), BF)),
             in_specs=[hbm] * 7 + [pl.BlockSpec(memory_space=pltpu.SMEM)],
             out_specs=(vmem, vmem, vmem),

time: 66.5 us -> 56.9 us (0.86)
  Pallas kernels: 63 us -> 53 us
    pallas_call x1, Pallas kernels: 63 us -> 53 us  [local(): pl.pallas_call(_kernel, out_shape=(pltpu.VMEM((2, ne // 2, nm, bl, d), BF...]
where the time goes in v3:
time: 56.9 us; the launch traced here: 56.4 us
  Pallas kernels  53 us (93%)
  local copies, waits for them, and re-layouts  2.73 us (5%)
  between operations  0.64 us (1%)
    pallas_call x1, Pallas kernels, local(): pl.pallas_call(_kernel, out_shape=(pltpu.VMEM((2, ne // 2, nm, bl, d), BF...  53 us
    unnamed x3, local copies, waits for them, and re-layouts  2.73 us

profile of v3, /device:TPU:1, one launch (start us, length us, event | category | flops | bytes accessed | tf_op | source)
XLA Modules:
  0.0 56.4 jit_solution(722051860265471011)
XLA Ops:
  0.6 53.0 %shard_map.103 = (bf16[2,2,4,32,2048]{4,3,2,1,0:T(8,128)(2,1)S(1)}, bf16[512,256]{1,0:T(8,128)(2,1)S(1)}, bf16[512,256]{1,0:T(8,128)(2,1)S(1)}) custom-call(bf16[512,2048]{1,0:T(8,128)(2,1)} %x_h.1, bf16[512,512]{1,0:T(8,128)(2,1)} %wq_h.1, bf16[2048,256]{1,0:T(8,128)(2,1)} %wk_h.1, bf16[2048,256]{1,0:T(8,128)(2,1)} %wv_h.1, bf16[512,512]{1,0:T(8,128)(2,1)} %wo_h.1, ...), custom_call_target="tpu_custom_call" | custom-call | tf_op jit(solution)/shard_map/pallas_call | solution.py:455
  53.7 1.3 %copy.14 = bf16[512,2048]{1,0:T(8,128)(2,1)} copy(bf16[512,2048]{1,0:T(8,128)(2,1)S(1)} %bitcast.1) | data formatting | bytes 4194304
  55.0 0.7 %copy.15 = bf16[512,256]{1,0:T(8,128)(2,1)} copy(bf16[512,256]{1,0:T(8,128)(2,1)S(1)} %get-tuple-element.10) | data formatting | bytes 524288
  55.7 0.7 %copy.16 = bf16[512,256]{1,0:T(8,128)(2,1)} copy(bf16[512,256]{1,0:T(8,128)(2,1)S(1)} %get-tuple-element.11) | data formatting | bytes 524288

commit v4 on v3

--- a/solution.py
+++ b/solution.py
@@ -189,6 +189,10 @@
     w_z(0).start()
     w_y(0).start()
 
+    @pl.when(~far)
+    def _():
+        w_y(1).start()
+
     ld_x.wait()
     ld_wk.wait()
     ld_wv.wait()
@@ -237,25 +241,45 @@
         a_rec(zs).wait_recv()
         x_fwd(zs).start()
     w_z(1).start()
+    w_pass_z(0)
     for zs in (near, z2, 3 - z):
         x_rec(zs).wait_recv()
         qacc[...] += qdot(zs)
     q_my[...] = qacc[...].astype(BF).reshape(q_my.shape)
 
     slot = (4 * yy + z) * 2 + c
-    for k in range(1, 16):
+    qh = bl // 2
+
+    def q_copy(hf, k):
         p = lax.rem(me + k, 16)
-        rcopy(q_my.at[p], q_in.at[slot], c_s.at[k - 1], c_r.at[slot], r, p // 4, p % 4).start()
+        rows = pl.ds(hf * qh, qh)
+        return rcopy(q_my.at[p, rows, :], q_in.at[slot, rows, :], c_s.at[hf, k - 1], c_r.at[hf, slot],
+                     r, p // 4, p % 4)
+
+    for hf in range(2):
+        for k in range(1, 16):
+            q_copy(hf, k).start()
     q_in[slot] = q_my[me]
 
-    w_pass_z(0)
+    def q_wait(hf):
+        rows = pl.ds(hf * qh, qh)
+        for k in range(1, 16):
+            s_ = lax.rem(slot + k, 16)
+            rcopy(q_in.at[s_, rows, :], q_in.at[s_, rows, :], c_s.at[hf, k - 1], c_r.at[hf, s_],
+                  r, z, m).wait_recv()
+        for s_ in range(16):
+            qf[s_ * bl + hf * qh:s_ * bl + (hf + 1) * qh, :] = (
+                q_in[s_, hf * qh:(hf + 1) * qh, :].astype(F32))
+
     w_pass_z(1)
-    w_y(1).start()
-
-    for k in range(1, 16):
-        s_ = lax.rem(slot + k, 16)
-        rcopy(q_in.at[s_], q_in.at[s_], c_s.at[k - 1], c_r.at[s_], r, z, m).wait_recv()
-    qf[...] = q_in[...].astype(F32).reshape(qf.shape)
+
+    @pl.when(far)
+    def _():
+        w_y(1).start()
+
+    w_pass_y(0)
+
+    q_wait(0)
 
     lane = lax.broadcasted_iota(jnp.int32, (nh, t), 1)
 
@@ -281,16 +305,6 @@
         of[0, pl.ds(bb, nh, stride=nb), :] = o[:, :half]
         of[1, pl.ds(bb, nh, stride=nb), :] = o[:, half:]
 
-    def attend(base):
-        s, p = {}, {}
-        for i in range(nb + 2 * LAG):
-            if i < nb:
-                s[i] = scores(base + i)
-            if LAG <= i < nb + LAG:
-                p[i - LAG] = weights(base + i - LAG, s.pop(i - LAG))
-            if i >= 2 * LAG:
-                values(base + i - 2 * LAG, i - 2 * LAG, *p.pop(i - 2 * LAG))
-
     pos = z // 2
     og = pos * 2 + c
 
@@ -318,6 +332,15 @@
 
     def yz_send(n, k):
         return rcopy(blk(n, z, m), blk(n, z, m), yz_s.at[n, k], yz_r.at[n, z], r, others[k], m)
+
+    inner = (z == 1) | (z == 2)
+    ii = lax.rem((z + 1) // 2, 2)
+    arrive = (near + ii * (others[1] - near), others[2] + ii * (near - others[2]),
+              others[1] + ii * (others[2] - others[1]))
+
+    def yz_pass(n):
+        zs = others[1]
+        return rcopy(blk(n, zs, m), blk(n, zs, m), yz_s.at[n, 3], yz_r.at[n, zs], r, near, m)
 
     def yz_rec(n, zs):
         return rcopy(blk(n, zs, m), blk(n, zs, m), yz_s.at[n, 0], yz_r.at[n, zs], r, near, m)
@@ -344,11 +367,10 @@
         o_rec(n, pos * 2 + 1 - c).wait_recv()
         o_rec(n, (1 - pos) * 2 + 1 - c).wait_recv()
         ob = [o_in[n, g].astype(F32) for g in range(4)]
-        acc = jnp.zeros((4 * nb, de), F32)
-        for h in range(nh):
-            lhs = jnp.concatenate([ob[g][h * nb:(h + 1) * nb] for g in range(4)], axis=0).astype(BF)
-            acc = acc + jnp.dot(lhs, wo_v[h // 2, (h % 2) * dh:(h % 2 + 1) * dh, :],
-                                preferred_element_type=F32)
+        lhs = jnp.concatenate(
+            [jnp.concatenate([ob[g][h * nb:(h + 1) * nb] for g in range(4)], axis=0).astype(BF)
+             for h in range(nh)], axis=1)
+        acc = jnp.dot(lhs, wo_v[...].reshape(nh * dh, de), preferred_element_type=F32)
         cols = pl.ds(pl.multiple_of((2 * (z // 2) + c) * de, de), de)
         for g in range(4):
             mm = 2 * yy + g % 2
@@ -356,8 +378,12 @@
             xr = x_v[pl.ds(pl.multiple_of(row, bl), bl), cols].astype(F32)
             yb = xr[n * nb:(n + 1) * nb] + acc[g * nb:(g + 1) * nb]
             y_v[g // 2, z % 2, mm, n * nb:(n + 1) * nb, cols] = yb.astype(BF)
-        for k in (2, 1, 0):
-            yz_send(n, k).start()
+        @pl.when(~inner)
+        def _():
+            yz_send(n, 2).start()
+
+        yz_send(n, 1).start()
+        yz_send(n, 0).start()
         yy_send(n, z).start()
         yd_send(n, z, 0).start()
 
@@ -366,8 +392,12 @@
         yd_send(n, zs, 0).start()
 
     def drain_z(n):
-        for zs in others:
+        for k, zs in enumerate(arrive):
             yz_rec(n, zs).wait_recv()
+            if k == 0:
+                @pl.when(inner)
+                def _():
+                    yz_pass(n).start()
             spread(n, zs)
 
     def drain_y(n):
@@ -375,18 +405,29 @@
             yy_rec(n, zs).wait_recv()
             yd_send(n, zs, 1).start()
 
-    for n in range(NB):
-        for i in range(n * nb // CHUNK, (n + 1) * nb // CHUNK):
-            kcp[i].wait()
-            vcp[i].wait()
-        attend(n * nb)
-        o_in[n, og] = jnp.concatenate([of[0], of[1]], axis=1).astype(BF)
-        o_send(n, 1).start()
-        o_send(n, 0).start()
-        if n > 1:
-            o_mid(n - 2)
-        if n < 2:
-            w_pass_y(n)
+    s, p = {}, {}
+    for i in range(bl + 2 * LAG):
+        if i < bl:
+            if i == qh:
+                q_wait(1)
+            if i % CHUNK == 0:
+                kcp[i // CHUNK].wait()
+                vcp[i // CHUNK].wait()
+            s[i] = scores(i)
+        if LAG <= i < bl + LAG:
+            p[i - LAG] = weights(i - LAG, s.pop(i - LAG))
+        if i >= 2 * LAG:
+            b = i - 2 * LAG
+            values(b, b % nb, *p.pop(b))
+            if (b + 1) % nb == 0:
+                n = b // nb
+                o_in[n, og] = jnp.concatenate([of[0], of[1]], axis=1).astype(BF)
+                o_send(n, 1).start()
+                o_send(n, 0).start()
+                if n > 1:
+                    o_mid(n - 2)
+                if n == 0:
+                    w_pass_y(1)
 
     w_wait()
     project(0)
@@ -397,10 +438,10 @@
     project(3)
     drain_z(0)
     drain_z(1)
+    drain_z(2)
+    drain_z(3)
     drain_y(0)
-    drain_z(2)
     drain_y(1)
-    drain_z(3)
     drain_y(2)
     drain_y(3)
     for n in range(NB):
@@ -411,9 +452,9 @@
     a_each(lambda d, own: None if own else d.wait_send())
     for k in range(1, 4):
         x_fwd(lax.rem(z + k, 4)).wait_send()
-    for k in range(1, 16):
-        p = lax.rem(me + k, 16)
-        rcopy(q_my.at[p], q_in.at[slot], c_s.at[k - 1], c_r.at[slot], r, p // 4, p % 4).wait_send()
+    for hf in range(2):
+        for k in range(1, 16):
+            q_copy(hf, k).wait_send()
     @pl.when(far)
     def _():
         w_d2d.wait_send()
@@ -430,12 +471,31 @@
         for k in range(2):
             o_send(n, k).wait_send()
         o_pass(n).wait_send()
-        for k in range(3):
-            yz_send(n, k).wait_send()
+        yz_send(n, 0).wait_send()
+        yz_send(n, 1).wait_send()
+
+        @pl.when(~inner)
+        def _():
+            yz_send(n, 2).wait_send()
+
+        @pl.when(inner)
+        def _():
+            yz_pass(n).wait_send()
+
         for zs in range(4):
             yy_send(n, zs).wait_send()
             yd_send(n, zs, 0).wait_send()
             yd_send(n, zs, 1).wait_send()
+
+
+def _store(y_v, kn_v, vn_v, y_h, kn_h, vn_h, sem):
+    copies = [pltpu.make_async_copy(y_v, y_h, sem.at[0]),
+              pltpu.make_async_copy(kn_v, kn_h, sem.at[1]),
+              pltpu.make_async_copy(vn_v, vn_h, sem.at[2])]
+    for copy in copies:
+        copy.start()
+    for copy in copies:
+        copy.wait()
 
 
 def solution(mesh):
@@ -470,16 +530,24 @@
                 pltpu.VMEM((2, nh * nb, dh // 2), F32),
                 pltpu.VMEM((NB, 4, nh * nb, dh), BF),
                 dma((6,)), dma((bl // CHUNK,)), dma((bl // CHUNK,)),
-                dma((4,)), dma((4,)), dma((4,)), dma((4,)), dma((15,)), dma((16,)),
+                dma((4,)), dma((4,)), dma((4,)), dma((4,)), dma((2, 15)), dma((2, 16)),
                 dma((1,)), dma((1,)), dma((2,)), dma((2,)), dma((2, 2)), dma((4, 2)),
                 dma((4, 2)), dma((4, 2)),
-                dma((NB, 3)), dma((NB, 4)), dma((NB, 3)), dma((NB, 4)),
+                dma((NB, 3)), dma((NB, 4)), dma((NB, 4)), dma((NB, 4)),
                 dma((NB, 4)), dma((NB, 4)), dma((NB, 2, 4)), dma((NB, 2, 4)),
             ],
             compiler_params=pltpu.CompilerParams(
                 collective_id=0, has_side_effects=True, vmem_limit_bytes=VMEM_LIMIT),
         )(x, Wq, Wk, Wv, Wo, Kc, Vc, lengths)
-        return y.reshape(b, d), kn, vn
+        y, kn, vn = (pltpu.with_memory_space_constraint(a, pltpu.VMEM) for a in (y.reshape(b, d), kn, vn))
+        return pl.pallas_call(
+            _store,
+            out_shape=(jax.ShapeDtypeStruct((b, d), BF), jax.ShapeDtypeStruct((b, dh), BF),
+                       jax.ShapeDtypeStruct((b, dh), BF)),
+            in_specs=[vmem] * 3,
+            out_specs=(hbm, hbm, hbm),
+            scratch_shapes=[dma((3,))],
+        )(y, kn, vn)
 
     in_specs = (P('rep', None), P('emb', 'model'), P(), P(), P('model', 'emb'),
                 P('rep', None, None), P('rep', None, None), P('rep'))

time: 56.9 us -> 55.2 us (0.970)
  local copies, waits for them, and re-layouts: 2.73 us -> 0 us
  Pallas kernels: 53 us -> 54.4 us
    unnamed x3 -> x0, local copies, waits for them, and re-layouts: 2.73 us -> none
    pallas_call x0 -> x1, Pallas kernels: none -> 1.51 us  [local(): pl.pallas_call(_store, out_shape=(jax.ShapeDtypeStruct((b, d), BF), jax.S...]
where the time goes in v4:
time: 55.2 us; the launch traced here: 55.1 us
  Pallas kernels  54.4 us (99%)
  between operations  0.64 us (1%)
    pallas_call x1, Pallas kernels, local(): pl.pallas_call(_kernel, out_shape=(pltpu.VMEM((2, ne // 2, nm, bl, d), BF...  52.9 us
    pallas_call x1, Pallas kernels, local(): pl.pallas_call(_store, out_shape=(jax.ShapeDtypeStruct((b, d), BF), jax.S...  1.51 us

profile of v4, /device:TPU:1, one launch (start us, length us, event | category | flops | bytes accessed | tf_op | source)
XLA Modules:
  0.0 55.1 jit_solution(11956905688635421740)
XLA Ops:
  0.6 52.9 %shard_map.103 = (bf16[2,2,4,32,2048]{4,3,2,1,0:T(8,128)(2,1)S(1)}, bf16[512,256]{1,0:T(8,128)(2,1)S(1)}, bf16[512,256]{1,0:T(8,128)(2,1)S(1)}) custom-call(bf16[512,2048]{1,0:T(8,128)(2,1)} %x_h.1, bf16[512,512]{1,0:T(8,128)(2,1)} %wq_h.1, bf16[2048,256]{1,0:T(8,128)(2,1)} %wk_h.1, bf16[2048,256]{1,0:T(8,128)(2,1)} %wv_h.1, bf16[512,512]{1,0:T(8,128)(2,1)} %wo_h.1, ...), custom_call_target="tpu_custom_call" | custom-call | tf_op jit(solution)/shard_map/pallas_call | solution.py:515
  53.6 1.5 %shard_map.104 = (bf16[512,2048]{1,0:T(8,128)(2,1)}, bf16[512,256]{1,0:T(8,128)(2,1)}, bf16[512,256]{1,0:T(8,128)(2,1)}) custom-call(bf16[512,2048]{1,0:T(8,128)(2,1)S(1)} %bitcast.1, bf16[512,256]{1,0:T(8,128)(2,1)S(1)} %get-tuple-element.7.kn_v, bf16[512,256]{1,0:T(8,128)(2,1)S(1)} %get-tuple-element.8.vn_v), custom_call_target="tpu_custom_call" | custom-call | tf_op jit(solution)/shard_map/pallas_call | solution.py:543

commit v5 on v4

--- a/solution.py
+++ b/solution.py
@@ -76,22 +76,26 @@
     pl.semaphore_wait(barrier, 16)
 
     ld_wq.wait()
-    ld_wq_rows = pl.ds(pl.multiple_of(r * hr, hr), hr)
-
-    def a_half(tt, cd, i):
+    hq = hr // 2
+
+    def quarter(g, j):
+        return pl.ds(pl.multiple_of(g * hr + j * hq, hq), hq)
+
+    def a_half(tt, cd, i, j):
         zd = 2 * c + tt
         cols = pl.ds(tt * dh + cd * half, half)
-        return rcopy(wq_v.at[ld_wq_rows, cols], wall.at[z, ld_wq_rows, :], a_s.at[i], a_r.at[z],
+        rows = quarter(r, j)
+        return rcopy(wq_v.at[rows, cols], wall.at[z, rows, :], a_s.at[i, j], a_r.at[z, j],
                      r, zd, yy * 2 + cd)
 
     def a_full(tt, cd, i):
         cols = pl.ds(tt * dh + cd * half, half)
-        return rcopy(wq_v.at[:, cols], wall.at[z], a_s.at[i], a_r.at[z],
+        return rcopy(wq_v.at[:, cols], wall.at[z], a_s.at[i, 0], a_r.at[z, 0],
                      r, z, yy * 2 + cd)
 
     def a_self(tt, cd, i):
         cols = pl.ds(tt * dh + cd * half, half)
-        return pltpu.make_async_copy(wq_v.at[:, cols], wall.at[z], a_s.at[i])
+        return pltpu.make_async_copy(wq_v.at[:, cols], wall.at[z], a_s.at[i, 0])
 
     def a_each(fn):
         for first in range(2):
@@ -104,7 +108,8 @@
 
                         @pl.when(zd != z)
                         def _():
-                            fn(a_half(tt, cd, i), False)
+                            fn(a_half(tt, cd, i, 0), False)
+                            fn(a_half(tt, cd, i, 1), False)
 
                         @pl.when((zd == z) & (c != cd))
                         def _():
@@ -186,7 +191,6 @@
     def _():
         w_own.start()
 
-    w_z(0).start()
     w_y(0).start()
 
     @pl.when(~far)
@@ -206,19 +210,17 @@
 
     ms = yy * 2 + z // 2
 
-    def a_rec(zs):
-        return rcopy(wall.at[zs, ld_wq_rows, :], wall.at[zs, ld_wq_rows, :], a_s.at[0], a_r.at[zs],
-                     r, zs, ms)
-
-    def x_fwd(zs):
-        return rcopy(wall.at[zs, ld_wq_rows, :], wall.at[zs, ld_wq_rows, :], x_s.at[zs], x_r.at[zs],
-                     1 - r, z, m)
-
-    other = pl.ds(pl.multiple_of((1 - r) * hr, hr), hr)
-
-    def x_rec(zs):
-        return rcopy(wall.at[zs, other, :], wall.at[zs, other, :], x_s.at[zs], x_r.at[zs],
-                     1 - r, z, m)
+    def a_rec(zs, j):
+        part = wall.at[zs, quarter(r, j), :]
+        return rcopy(part, part, a_s.at[0, 0], a_r.at[zs, j], r, zs, ms)
+
+    def x_fwd(zs, j):
+        part = wall.at[zs, quarter(r, j), :]
+        return rcopy(part, part, x_s.at[zs, j], x_r.at[zs, j], 1 - r, z, m)
+
+    def x_rec(zs, j):
+        part = wall.at[zs, quarter(1 - r, j), :]
+        return rcopy(part, part, x_s.at[zs, j], x_r.at[zs, j], 1 - r, z, m)
 
     def qdot(zs):
         cols = pl.ds(pl.multiple_of(zs * de, de), de)
@@ -234,16 +236,20 @@
 
     @pl.when(ms != m)
     def _():
-        rcopy(wall.at[z], wall.at[z], a_s.at[0], a_r.at[z], r, z, my).wait_recv()
+        rcopy(wall.at[z], wall.at[z], a_s.at[0, 0], a_r.at[z, 0], r, z, my).wait_recv()
 
     qacc[...] = qdot(z)
     for zs in (near, z2, 3 - z):
-        a_rec(zs).wait_recv()
-        x_fwd(zs).start()
+        for j in range(2):
+            a_rec(zs, j).wait_recv()
+            x_fwd(zs, j).start()
+        if zs is near:
+            w_z(0).start()
     w_z(1).start()
     w_pass_z(0)
     for zs in (near, z2, 3 - z):
-        x_rec(zs).wait_recv()
+        x_rec(zs, 0).wait_recv()
+        x_rec(zs, 1).wait_recv()
         qacc[...] += qdot(zs)
     q_my[...] = qacc[...].astype(BF).reshape(q_my.shape)
 
@@ -451,7 +457,8 @@
 
     a_each(lambda d, own: None if own else d.wait_send())
     for k in range(1, 4):
-        x_fwd(lax.rem(z + k, 4)).wait_send()
+        for j in range(2):
+            x_fwd(lax.rem(z + k, 4), j).wait_send()
     for hf in range(2):
         for k in range(1, 16):
             q_copy(hf, k).wait_send()
@@ -530,7 +537,7 @@
                 pltpu.VMEM((2, nh * nb, dh // 2), F32),
                 pltpu.VMEM((NB, 4, nh * nb, dh), BF),
                 dma((6,)), dma((bl // CHUNK,)), dma((bl // CHUNK,)),
-                dma((4,)), dma((4,)), dma((4,)), dma((4,)), dma((2, 15)), dma((2, 16)),
+                dma((4, 2)), dma((4, 2)), dma((4, 2)), dma((4, 2)), dma((2, 15)), dma((2, 16)),
                 dma((1,)), dma((1,)), dma((2,)), dma((2,)), dma((2, 2)), dma((4, 2)),
                 dma((4, 2)), dma((4, 2)),
                 dma((NB, 3)), dma((NB, 4)), dma((NB, 4)), dma((NB, 4)),

time: 55.2 us -> 55.1 us (level)
  no operation moved by 1% of the time
where the time goes in v5:
time: 55.1 us; the launch traced here: 55 us
  Pallas kernels  54.3 us (99%)
  between operations  0.64 us (1%)
    pallas_call x1, Pallas kernels, local(): pl.pallas_call(_kernel, out_shape=(pltpu.VMEM((2, ne // 2, nm, bl, d), BF...  52.8 us
    pallas_call x1, Pallas kernels, local(): pl.pallas_call(_store, out_shape=(jax.ShapeDtypeStruct((b, d), BF), jax.S...  1.51 us

profile of v5, /device:TPU:1, one launch (start us, length us, event | category | flops | bytes accessed | tf_op | source)
XLA Modules:
  0.0 55.0 jit_solution(3442729223509029310)
XLA Ops:
  0.6 52.8 %shard_map.103 = (bf16[2,2,4,32,2048]{4,3,2,1,0:T(8,128)(2,1)S(1)}, bf16[512,256]{1,0:T(8,128)(2,1)S(1)}, bf16[512,256]{1,0:T(8,128)(2,1)S(1)}) custom-call(bf16[512,2048]{1,0:T(8,128)(2,1)} %x_h.1, bf16[512,512]{1,0:T(8,128)(2,1)} %wq_h.1, bf16[2048,256]{1,0:T(8,128)(2,1)} %wk_h.1, bf16[2048,256]{1,0:T(8,128)(2,1)} %wv_h.1, bf16[512,512]{1,0:T(8,128)(2,1)} %wo_h.1, ...), custom_call_target="tpu_custom_call" | custom-call | tf_op jit(solution)/shard_map/pallas_call | solution.py:522
  53.4 1.5 %shard_map.104 = (bf16[512,2048]{1,0:T(8,128)(2,1)}, bf16[512,256]{1,0:T(8,128)(2,1)}, bf16[512,256]{1,0:T(8,128)(2,1)}) custom-call(bf16[512,2048]{1,0:T(8,128)(2,1)S(1)} %bitcast.1, bf16[512,256]{1,0:T(8,128)(2,1)S(1)} %get-tuple-element.7.kn_v, bf16[512,256]{1,0:T(8,128)(2,1)S(1)} %get-tuple-element.8.vn_v), custom_call_target="tpu_custom_call" | custom-call | tf_op jit(solution)/shard_map/pallas_call | solution.py:550
